TPU v7x, 32 devices: a whole 2x2x4 slice. The times are simulated.
32 devices in a mesh: row: 4 (over y, core), col: 8 (over z, x).
Axes of the slice: x: 2, y: 2, z: 4, core: 2. Of those that a mesh axis runs over, the one named last changes fastest.
Arguments:
- rhs: bfloat16 [6144, 6144], P('row', 'col'), may hold values from -6 to 6
- basis_left: bfloat16 [6144, 6144], P('col', 'row'), may hold values from -1 to 1, as said below
- basis_right: bfloat16 [6144, 6144], P('row', 'col'), may hold values from -1 to 1, as said below
- eig_left: float32 [6144], P('row'), may hold values from 0.1 to 4
- eig_right: float32 [6144], P('col'), may hold values from 0.1 to 4
Outputs:
- solution: bfloat16 [6144, 6144], P('col', 'row')
Inputs may be any that keep to these rules, and one draw needn't show every extreme that they name: `basis_left`: an orthogonal matrix drawn uniformly, rounded to bfloat16. `basis_right`: an orthogonal matrix drawn uniformly, rounded to bfloat16.
All inputs are finite; a program needn't handle non-finite values.
Results may differ from a plain program's by a relative error of at most 0.0085.
Values may be sent and summed in bfloat16 or wider, within the bound.
A program may use at most 128 MiB of HBM per device.

v0:
```python
import jax
import jax.numpy as jnp
from jax import lax
from jax.sharding import PartitionSpec as P


def body(rhs, basis_left, basis_right, eig_left, eig_right):
    c_strip = lax.all_gather(rhs, "row", axis=0, tiled=True)
    left_all = lax.all_gather(basis_left, "col", axis=0, tiled=True)
    first = lax.dot_general(
        left_all, c_strip, (((0,), (0,)), ((), ())), preferred_element_type=jnp.float32
    )
    projected = first.astype(jnp.bfloat16)
    right_strip = lax.all_gather(basis_right, "row", axis=0, tiled=True)
    chosen = right_strip
    second = jnp.dot(
        lax.all_gather(projected, "col", axis=1, tiled=True),
        chosen,
        preferred_element_type=jnp.float32,
    )
    scaled = (second / (eig_left[:, None] + eig_right[None, :])).astype(jnp.bfloat16)
    chosen = left_all
    half = lax.psum_scatter(
        jnp.dot(chosen, scaled, preferred_element_type=jnp.float32),
        "row",
        scatter_dimension=0,
        tiled=True,
    ).astype(jnp.bfloat16)
    half_all = lax.all_gather(half, "row", axis=0, tiled=True)
    chosen = half_all
    return lax.psum_scatter(
        lax.dot_general(
            chosen, basis_right, (((1,), (1,)), ((), ())), preferred_element_type=jnp.float32
        ),
        "col",
        scatter_dimension=0,
        tiled=True,
    ).astype(jnp.bfloat16)


def solution(mesh):
    in_specs = (P("row", "col"), P("col", "row"), P("row", "col"), P("row"), P("col"))
    out_specs = P("col", "row")
    return jax.shard_map(body, mesh=mesh, in_specs=in_specs, out_specs=out_specs, check_vma=False)
```

profile of v0, /device:TPU:0, one launch (start us, length us, event | category | flops | bytes accessed | tf_op | source)
XLA Modules:
  0.0 1751.5 jit_solution(14869084896472922109)
XLA Ops:
  6.5 0.7 all-gather.8.cloned.1.call-update
  7.3 0.0 all-gather.6.cloned.1.call-start
  7.3 0.7 all-gather.6.cloned.1.call-update
  8.0 0.0 all-gather.12.cloned.1.call-start
  8.1 0.7 all-gather.12.cloned.1.call-update
  8.8 0.0 all-gather.10.cloned.1.call-start
  8.8 67.1 %all-gather.8.cloned.1.call-done = bf16[6144,768]{1,0:T(8,128)(2,1)} async-done(((bf16[1536,768]{1,0:T(8,128)(2,1)}), bf16[6144,768]{1,0:T(8,128)(2,1)}) %all-gather.8.cloned.1.call-update) | async-done | bytes 9437200 | tf_op jit(solution)/shard_map/all_gather | solution.py:8
  75.9 364.0 %all-gather.6.cloned.1.call-done = bf16[6144,1536]{1,0:T(8,128)(2,1)} async-done(((bf16[768,1536]{1,0:T(8,128)(2,1)}), bf16[6144,1536]{1,0:T(8,128)(2,1)}) %all-gather.6.cloned.1.call-update) | async-done | bytes 18874384 | tf_op jit(solution)/shard_map/all_gather | solution.py:9
  439.8 21.5 %convolution_convert_fusion = bf16[1536,768]{1,0:T(8,128)(2,1)} fusion(bf16[6144,1536]{1,0:T(8,128)(2,1)} %all-gather.6.cloned.1.call-done, bf16[6144,768]{1,0:T(8,128)(2,1)} %all-gather.8.cloned.1.call-done), kind=kOutput, calls=%fused_computation.2 | convolution fusion | flops 14496694272 | bytes 30670848 | tf_op jit(solution)/shard_map/dot_general | solution.py:10
  461.3 0.0 all-gather.10.cloned.1.call-update
  461.3 0.2 reduce-scatter.3.cloned.1.call-start
  461.5 44.1 %all-gather.12.cloned.1.call-done = bf16[6144,768]{1,0:T(8,128)(2,1)} async-done(((bf16[1536,768]{1,0:T(8,128)(2,1)}), bf16[6144,768]{1,0:T(8,128)(2,1)}) %all-gather.12.cloned.1.call-update) | async-done | bytes 9437200 | tf_op jit(solution)/shard_map/all_gather | solution.py:14
  505.6 363.8 %all-gather.10.cloned.1.call-done = bf16[1536,6144]{1,0:T(8,128)(2,1)} async-done(((bf16[1536,768]{1,0:T(8,128)(2,1)}), bf16[1536,6144]{1,0:T(8,128)(2,1)}) %all-gather.10.cloned.1.call-update) | async-done | bytes 18874384 | tf_op jit(solution)/shard_map/all_gather | solution.py:17
  869.4 20.6 %divide_convert_fusion = bf16[1536,768]{1,0:T(8,128)(2,1)S(1)} fusion(bf16[1536,6144]{1,0:T(8,128)(2,1)} %all-gather.10.cloned.1.call-done, bf16[6144,768]{1,0:T(8,128)(2,1)} %all-gather.12.cloned.1.call-done, f32[768]{0:T(1024)S(1)} %copy-done.2, f32[1536]{0:T(1024)S(1)} %copy-done.1), kind=kOutput, calls=%fused_computation.1 | convolution fusion | flops 14499053568 | bytes 30680064 | tf_op jit(solution)/shard_map/dot_general | solution.py:16
  890.1 20.7 %convolution_bitcast_fusion = f32[6144,768]{0,1:T(8,128)} fusion(bf16[1536,768]{1,0:T(8,128)(2,1)S(1)} %divide_convert_fusion, bf16[6144,1536]{1,0:T(8,128)(2,1)} %all-gather.6.cloned.1.call-done), kind=kOutput, calls=%fused_computation | convolution fusion | flops 14495514624 | bytes 40108032 | tf_op jit(solution)/shard_map/dot_general | solution.py:24
  910.8 0.0 all-gather.14.cloned.1.call-start
  910.9 137.8 %reduce-scatter.3.cloned.1.call-done = f32[1536,768]{0,1:T(8,128)} async-done(((f32[6144,768]{0,1:T(8,128)}), f32[1536,768]{0,1:T(8,128)}) %reduce-scatter.3.cloned.1.call-update) | async-done | bytes 4718608 | tf_op jit(solution)/shard_map/reduce_scatter | solution.py:23
  1048.7 4.0 convert_element_type.14
  1052.7 0.0 all-gather.14.cloned.1.call-update
  1052.7 0.3 reduce-scatter.5.cloned.1.call-start
  1053.0 64.1 %all-gather.14.cloned.1.call-done = bf16[6144,768]{0,1:T(8,128)(2,1)} async-done(((bf16[1536,768]{0,1:T(8,128)(2,1)}), bf16[6144,768]{0,1:T(8,128)(2,1)}) %all-gather.14.cloned.1.call-update) | async-done | bytes 9437200 | tf_op jit(solution)/shard_map/all_gather | solution.py:29
  1117.1 22.7 %fusion = f32[6144,1536]{1,0:T(8,128)} fusion(bf16[6144,768]{0,1:T(8,128)(2,1)} %all-gather.14.cloned.1.call-done, bf16[1536,768]{1,0:T(8,128)(2,1)S(1)} %copy-done), kind=kOutput, calls=%fused_computation.3 | convolution fusion | flops 14495514624 | bytes 49545216 | tf_op jit(solution)/shard_map/dot_general | solution.py:32
  1139.8 600.8 %reduce-scatter.5.cloned.1.call-done = f32[768,1536]{1,0:T(8,128)} async-done(((f32[6144,1536]{1,0:T(8,128)}), f32[768,1536]{1,0:T(8,128)}) %reduce-scatter.5.cloned.1.call-update) | async-done | bytes 4718608 | tf_op jit(solution)/shard_map/reduce_scatter | solution.py:31
  1740.6 4.0 convert_element_type.15
  (9 shorter events, 0.0 us)
Async XLA Ops:
  6.5 69.3 %all-gather.8.cloned.1.call-start = ((), (), s32[]{:S(2)}) async-start(), calls=%async_computation.3 | async-start | bytes 11796480 | tf_op jit(solution)/shard_map/all_gather | solution.py:8
  7.3 432.6 %all-gather.6.cloned.1.call-start = ((), (), s32[]{:S(2)}) async-start(), calls=%async_computation.2 | async-start | bytes 21233664 | tf_op jit(solution)/shard_map/all_gather | solution.py:9
  8.0 497.6 %all-gather.12.cloned.1.call-start = ((), (), s32[]{:S(2)}) async-start(), calls=%async_computation.5 | async-start | bytes 11796480 | tf_op jit(solution)/shard_map/all_gather | solution.py:14
  8.7 860.7 %copy-start.1 = (f32[1536]{0:T(1024)S(1)}, f32[1536]{0:T(1024)}, u32[]{:S(2)}) copy-start(f32[1536]{0:T(1024)} %param.8) | copy-start | bytes 18436
  8.8 860.7 %copy-start.2 = (f32[768]{0:T(1024)S(1)}, f32[768]{0:T(1024)}, u32[]{:S(2)}) copy-start(f32[768]{0:T(1024)} %param.9) | copy-start | bytes 9220
  8.8 860.7 %all-gather.10.cloned.1.call-start = ((), (), s32[]{:S(2)}) async-start(), calls=%async_computation.4 | async-start | bytes 21233664 | tf_op jit(solution)/shard_map/all_gather | solution.py:17
  461.3 587.4 %reduce-scatter.3.cloned.1.call-start = ((), (), s32[]{:S(2)}) async-start(), calls=%async_computation.6 | async-start | bytes 23592960 | tf_op jit(solution)/shard_map/reduce_scatter | solution.py:23
  910.8 206.3 %copy-start = (bf16[1536,768]{1,0:T(8,128)(2,1)S(1)}, bf16[1536,768]{1,0:T(8,128)(2,1)}, u32[]{:S(2)}) copy-start(bf16[1536,768]{1,0:T(8,128)(2,1)} %param.7) | copy-start | bytes 7077892
  910.8 206.3 %all-gather.14.cloned.1.call-start = ((), (), s32[]{:S(2)}) async-start(), calls=%async_computation.7 | async-start | bytes 11796480 | tf_op jit(solution)/shard_map/all_gather | solution.py:29
  1052.7 687.9 %reduce-scatter.5.cloned.1.call-start = ((), (), s32[]{:S(2)}) async-start(), calls=%async_computation.8 | async-start | bytes 42467328 | tf_op jit(solution)/shard_map/reduce_scatter | solution.py:31
Sparse Core Ops, SparseCore 0:
  8.9 66.9 all-gather.7
  77.4 362.3 all-gather.5
  441.4 64.1 all-gather.11
  507.0 362.3 all-gather.9
  910.9 137.7 reduce-scatter.2
  1052.8 64.2 all-gather.13
  1139.9 600.6 reduce-scatter.4
where the time goes:
time: 1750 us
  waiting for transfers between devices  1640 us (94%)
  matrix products  85.5 us (5%)
    reduce_scatter x1, waiting for transfers between devices, body(): lax.psum_scatter(lax.dot_general(chosen, basis_right, (((1,), (1,)), ((),...  601 us
    all_gather x1, waiting for transfers between devices, body(): left_all = lax.all_gather(basis_left, 'col', axis=0, tiled=True)  364 us
    all_gather x1, waiting for transfers between devices, body(): lax.all_gather(projected, 'col', axis=1, tiled=True)  364 us
    reduce_scatter x1, waiting for transfers between devices, body(): lax.psum_scatter(jnp.dot(chosen, scaled, preferred_element_type=jnp.float...  138 us
    all_gather x1, waiting for transfers between devices, body(): c_strip = lax.all_gather(rhs, 'row', axis=0, tiled=True)  67.1 us
    all_gather x1, waiting for transfers between devices, body(): half_all = lax.all_gather(half, 'row', axis=0, tiled=True)  64.1 us
    all_gather x1, waiting for transfers between devices, body(): right_strip = lax.all_gather(basis_right, 'row', axis=0, tiled=True)  44.1 us
  transfers between devices with their start and end apart: 7, of which 7 were waited for; matrix products, arithmetic and copies ran while one was open for 1% of the time, Pallas kernels for 0%

commit v1 on v0

--- a/solution.py
+++ b/solution.py
@@ -2,6 +2,12 @@
 import jax.numpy as jnp
 from jax import lax
 from jax.sharding import PartitionSpec as P
+
+
+def gather_blocks(value, mesh_axis, dim):
+    parts = lax.all_gather(value, mesh_axis, axis=0, tiled=False)
+    result = jnp.concatenate(parts, axis=dim)
+    return result
 
 
 def body(rhs, basis_left, basis_right, eig_left, eig_right):
@@ -13,11 +19,7 @@
     projected = first.astype(jnp.bfloat16)
     right_strip = lax.all_gather(basis_right, "row", axis=0, tiled=True)
     chosen = right_strip
-    second = jnp.dot(
-        lax.all_gather(projected, "col", axis=1, tiled=True),
-        chosen,
-        preferred_element_type=jnp.float32,
-    )
+    second = jnp.dot(gather_blocks(projected, "col", 1), chosen, preferred_element_type=jnp.float32)
     scaled = (second / (eig_left[:, None] + eig_right[None, :])).astype(jnp.bfloat16)
     chosen = left_all
     half = lax.psum_scatter(

time: 1750 us -> 1770 us (1.011)
  local copies, waits for them, and re-layouts: 0.01 us -> 24 us
    all_gather x0 -> x1, local copies, waits for them, and re-layouts: none -> 24 us  [gather_blocks(): parts = lax.all_gather(value, mesh_axis, axis=0, tiled=False)]
where the time goes in v1:
time: 1770 us
  waiting for transfers between devices  1640 us (93%)
  matrix products  85.7 us (5%)
  local copies, waits for them, and re-layouts  24 us (1%)
    reduce_scatter x1, waiting for transfers between devices, body(): lax.psum_scatter(lax.dot_general(chosen, basis_right, (((1,), (1,)), ((),...  601 us
    all_gather x1, waiting for transfers between devices, body(): left_all = lax.all_gather(basis_left, 'col', axis=0, tiled=True)  364 us
    all_gather x1, waiting for transfers between devices, gather_blocks(): parts = lax.all_gather(value, mesh_axis, axis=0, tiled=False)  362 us
    reduce_scatter x1, waiting for transfers between devices, body(): lax.psum_scatter(jnp.dot(chosen, scaled, preferred_element_type=jnp.float...  138 us
    all_gather x1, waiting for transfers between devices, body(): c_strip = lax.all_gather(rhs, 'row', axis=0, tiled=True)  67.8 us
    all_gather x1, waiting for transfers between devices, body(): half_all = lax.all_gather(half, 'row', axis=0, tiled=True)  64.1 us
    all_gather x1, waiting for transfers between devices, body(): right_strip = lax.all_gather(basis_right, 'row', axis=0, tiled=True)  41.6 us
  transfers between devices with their start and end apart: 7, of which 7 were waited for; matrix products, arithmetic and copies ran while one was open for 1% of the time, Pallas kernels for 0%

profile of v1, /device:TPU:0, one launch (start us, length us, event | category | flops | bytes accessed | tf_op | source)
XLA Modules:
  0.0 1772.0 jit_solution(18214648041656031868)
XLA Ops:
  6.5 0.7 all-gather.9.cloned.1.call-update
  7.3 0.0 all-gather.7.cloned.1.call-start
  7.3 0.7 all-gather.7.cloned.1.call-update
  8.0 0.0 all-gather.15.cloned.1.call-start
  8.1 67.8 %all-gather.9.cloned.1.call-done = bf16[6144,768]{1,0:T(8,128)(2,1)} async-done(((bf16[1536,768]{1,0:T(8,128)(2,1)}), bf16[6144,768]{1,0:T(8,128)(2,1)}) %all-gather.9.cloned.1.call-update) | async-done | bytes 9437200 | tf_op jit(solution)/shard_map/all_gather | solution.py:14
  75.9 364.0 %all-gather.7.cloned.1.call-done = bf16[6144,1536]{1,0:T(8,128)(2,1)} async-done(((bf16[768,1536]{1,0:T(8,128)(2,1)}), bf16[6144,1536]{1,0:T(8,128)(2,1)}) %all-gather.7.cloned.1.call-update) | async-done | bytes 18874384 | tf_op jit(solution)/shard_map/all_gather | solution.py:15
  439.8 21.5 %convolution_convert_fusion = bf16[1536,768]{1,0:T(8,128)(2,1)} fusion(bf16[6144,1536]{1,0:T(8,128)(2,1)} %all-gather.7.cloned.1.call-done, bf16[6144,768]{1,0:T(8,128)(2,1)} %all-gather.9.cloned.1.call-done), kind=kOutput, calls=%fused_computation.2 | convolution fusion | flops 14496694272 | bytes 30670848 | tf_op jit(solution)/shard_map/dot_general | solution.py:16
  461.3 0.0 all-gather.15.cloned.1.call-update
  461.3 0.0 all-gather.11.cloned.1.call-start
  461.4 0.5 all-gather.11.cloned.1.call-update
  461.9 0.2 reduce-scatter.3.cloned.1.call-start
  462.1 361.7 %all-gather.15.cloned.1.call-done = bf16[12288,768]{1,0:T(8,128)(2,1)} async-done(((bf16[1536,768]{1,0:T(8,128)(2,1)}), bf16[12288,768]{1,0:T(8,128)(2,1)}) %all-gather.15.cloned.1.call-update) | async-done | bytes 18874384 | tf_op jit(solution)/shard_map/all_gather | solution.py:8
  823.8 24.0 %copy.6 = bf16[8,1536,768]{1,2,0:T(8,128)(2,1)} copy(bf16[8,1536,768]{2,1,0:T(8,128)(2,1)} %bitcast.14) | data formatting | bytes 37748736 | tf_op jit(solution)/shard_map/all_gather | solution.py:8
  847.8 41.6 %all-gather.11.cloned.1.call-done = bf16[6144,768]{1,0:T(8,128)(2,1)} async-done(((bf16[1536,768]{1,0:T(8,128)(2,1)}), bf16[6144,768]{1,0:T(8,128)(2,1)}) %all-gather.11.cloned.1.call-update) | async-done | bytes 9437200 | tf_op jit(solution)/shard_map/all_gather | solution.py:20
  889.5 20.9 %divide_convert_fusion = bf16[1536,768]{1,0:T(8,128)(2,1)S(1)} fusion(bf16[1536,6144]{0,1:T(8,128)(2,1)} %bitcast.15, bf16[6144,768]{1,0:T(8,128)(2,1)} %all-gather.11.cloned.1.call-done, f32[768]{0:T(1024)S(1)} %copy-done.2, f32[1536]{0:T(1024)S(1)} %copy-done.1), kind=kOutput, calls=%fused_computation.1 | convolution fusion | flops 14499053568 | bytes 30680064 | tf_op jit(solution)/shard_map/dot_general | solution.py:22
  910.3 20.7 %convolution_bitcast_fusion = f32[6144,768]{0,1:T(8,128)} fusion(bf16[1536,768]{1,0:T(8,128)(2,1)S(1)} %divide_convert_fusion, bf16[6144,1536]{1,0:T(8,128)(2,1)} %all-gather.7.cloned.1.call-done), kind=kOutput, calls=%fused_computation | convolution fusion | flops 14495514624 | bytes 40108032 | tf_op jit(solution)/shard_map/dot_general | solution.py:26
  931.1 0.0 all-gather.13.cloned.1.call-start
  931.1 137.8 %reduce-scatter.3.cloned.1.call-done = f32[1536,768]{0,1:T(8,128)} async-done(((f32[6144,768]{0,1:T(8,128)}), f32[1536,768]{0,1:T(8,128)}) %reduce-scatter.3.cloned.1.call-update) | async-done | bytes 4718608 | tf_op jit(solution)/shard_map/reduce_scatter | solution.py:25
  1069.0 4.0 convert_element_type.14
  1073.0 0.3 reduce-scatter.5.cloned.1.call-start
  1073.3 64.1 %all-gather.13.cloned.1.call-done = bf16[6144,768]{0,1:T(8,128)(2,1)} async-done(((bf16[1536,768]{0,1:T(8,128)(2,1)}), bf16[6144,768]{0,1:T(8,128)(2,1)}) %all-gather.13.cloned.1.call-update) | async-done | bytes 9437200 | tf_op jit(solution)/shard_map/all_gather | solution.py:31
  1137.4 22.7 %fusion = f32[6144,1536]{1,0:T(8,128)} fusion(bf16[6144,768]{0,1:T(8,128)(2,1)} %all-gather.13.cloned.1.call-done, bf16[1536,768]{1,0:T(8,128)(2,1)S(1)} %copy-done), kind=kOutput, calls=%fused_computation.3 | convolution fusion | flops 14495514624 | bytes 49545216 | tf_op jit(solution)/shard_map/dot_general | solution.py:34
  1160.1 601.1 %reduce-scatter.5.cloned.1.call-done = f32[768,1536]{1,0:T(8,128)} async-done(((f32[6144,1536]{1,0:T(8,128)}), f32[768,1536]{1,0:T(8,128)}) %reduce-scatter.5.cloned.1.call-update) | async-done | bytes 4718608 | tf_op jit(solution)/shard_map/reduce_scatter | solution.py:33
  1761.2 4.0 convert_element_type.15
  (10 shorter events, 0.1 us)
Async XLA Ops:
  6.5 69.3 %all-gather.9.cloned.1.call-start = ((), (), s32[]{:S(2)}) async-start(), calls=%async_computation.3 | async-start | bytes 11796480 | tf_op jit(solution)/shard_map/all_gather | solution.py:14
  7.3 432.6 %all-gather.7.cloned.1.call-start = ((), (), s32[]{:S(2)}) async-start(), calls=%async_computation.2 | async-start | bytes 21233664 | tf_op jit(solution)/shard_map/all_gather | solution.py:15
  8.0 815.8 %all-gather.15.cloned.1.call-start = ((), (), s32[]{:S(2)}) async-start(), calls=%async_computation.8 | async-start | bytes 21233664 | tf_op jit(solution)/shard_map/all_gather | solution.py:8
  461.3 428.2 %all-gather.11.cloned.1.call-start = ((), (), s32[]{:S(2)}) async-start(), calls=%async_computation.4 | async-start | bytes 11796480 | tf_op jit(solution)/shard_map/all_gather | solution.py:20
  461.9 607.1 %reduce-scatter.3.cloned.1.call-start = ((), (), s32[]{:S(2)}) async-start(), calls=%async_computation.5 | async-start | bytes 23592960 | tf_op jit(solution)/shard_map/reduce_scatter | solution.py:25
  823.8 65.6 %copy-start.1 = (f32[1536]{0:T(1024)S(1)}, f32[1536]{0:T(1024)}, u32[]{:S(2)}) copy-start(f32[1536]{0:T(1024)} %param.8) | copy-start | bytes 18436
  823.8 65.6 %copy-start.2 = (f32[768]{0:T(1024)S(1)}, f32[768]{0:T(1024)}, u32[]{:S(2)}) copy-start(f32[768]{0:T(1024)} %param.9) | copy-start | bytes 9220
  931.1 206.3 %copy-start = (bf16[1536,768]{1,0:T(8,128)(2,1)S(1)}, bf16[1536,768]{1,0:T(8,128)(2,1)}, u32[]{:S(2)}) copy-start(bf16[1536,768]{1,0:T(8,128)(2,1)} %param.7) | copy-start | bytes 7077892
  931.1 206.3 %all-gather.13.cloned.1.call-start = ((), (), s32[]{:S(2)}) async-start(), calls=%async_computation.6 | async-start | bytes 11796480 | tf_op jit(solution)/shard_map/all_gather | solution.py:31
  1073.0 688.2 %reduce-scatter.5.cloned.1.call-start = ((), (), s32[]{:S(2)}) async-start(), calls=%async_computation.7 | async-start | bytes 42467328 | tf_op jit(solution)/shard_map/reduce_scatter | solution.py:33
Sparse Core Ops, SparseCore 0:
  8.9 66.9 all-gather.8
  77.4 362.3 all-gather.6
  461.4 362.3 all-gather.14
  825.2 64.1 all-gather.10
  931.2 137.7 reduce-scatter.2
  1073.1 64.1 all-gather.12
  1160.2 600.9 reduce-scatter.4
